TPU v7x, 32 devices: a whole 2x2x4 slice. The times are simulated.
32 devices in a mesh: dp: 2 (over core), rows: 4 (over y, x), heads: 4 (over z).
Axes of the slice: x: 2, y: 2, z: 4, core: 2. Of those that a mesh axis runs over, the one named last changes fastest.
Arguments:
- hidden: bfloat16 [2, 16, 2048], P('dp'), may hold values from -458.54834 to 458.54834
- norm_gain: float32 [1, 2048], replicated, may hold values from 0.25 to 1.75
- query_weight: bfloat16 [1, 2048, 4096], P(None, None, ('heads', 'rows')), may hold values from -0.125 to 0.125
- key_weight: bfloat16 [1, 2048, 4096], P(None, None, ('heads', 'rows')), may hold values from -0.125 to 0.125
- value_weight: bfloat16 [1, 2048, 4096], P(None, None, ('heads', 'rows')), may hold values from -0.125 to 0.125
- zgate_weight: bfloat16 [1, 2048, 4096], P(None, None, ('heads', 'rows')), may hold values from -0.125 to 0.125
- gate_weight: bfloat16 [1, 2, 2048, 4], P(None, None, None, 'heads'), may hold values from -0.125 to 0.125
- decay_rate: float32 [1, 4], P(None, 'heads'), may hold values from 0.005 to 0.5
- output_gain: float32 [1, 1024], P(None, 'rows'), may hold values from 0.25 to 1.75
- output_weight: bfloat16 [1, 4096, 2048], P(None, ('heads', 'rows')), may hold values from -0.09375 to 0.09375
- recurrent_state: float32 [1, 2, 4, 1024, 1024], P(None, 'dp', 'heads', 'rows'), may hold values from -6 to 6
- final_gain: float32 [2048], replicated, may hold values from 0.25 to 1.75
- vocab_weight: bfloat16 [2048, 131072], P(None, ('dp', 'rows', 'heads')), may hold values from -7.9549513 to 7.9549513
Outputs:
- next_state: float32 [1, 2, 4, 1024, 1024], P(None, 'dp', 'heads', 'rows')
- log_probs: float32 [2, 16, 131072], P(None, None, ('dp', 'rows', 'heads'))
All inputs are finite; a program needn't handle non-finite values.
Results may differ from a plain program's by a relative error of at most 0.0024.
The roundings to bfloat16 on the way count: a program that leaves them out, or rounds other values in their place, can miss the bound.
Values may be sent and summed in bfloat16 or wider, within the bound.
A program may use at most 64 MiB of HBM per device.

v0:
```python
import jax
import jax.numpy as jnp
from jax import lax
from jax.sharding import PartitionSpec as P

DK = 1024


epsilon = 1e-06


def joined(shard, axis, combine):
    everything = jax.tree.map(lambda part: lax.all_gather(part, axis), shard)
    first = jax.tree.map(lambda part: part[0], everything)

    def hop(k, so_far):
        return combine(so_far, jax.tree.map(lambda part: part[k], everything))

    return lax.fori_loop(1, lax.axis_size(axis), hop, first)


def rms_norm(values, gain):
    return values * lax.rsqrt(jnp.mean(values * values, axis=-1, keepdims=True) + epsilon) * gain


def layer_total(partial_value):
    return lax.psum(partial_value, ("rows", "heads"))


def merge_pair(first, second):
    peak = jnp.maximum(first[0], second[0])
    return (peak, first[1] * jnp.exp(first[0] - peak) + second[1] * jnp.exp(second[0] - peak))


def on_device(
    hidden,
    norm_gain,
    query_weight,
    key_weight,
    value_weight,
    zgate_weight,
    gate_weight,
    decay_rate,
    output_gain,
    output_weight,
    recurrent_state,
    final_gain,
    vocab_weight,
):
    highest_score = lax.Precision.HIGHEST
    seq_count, tokens, model_width = hidden.shape
    stream = hidden.astype(jnp.float32)
    positions = jnp.arange(tokens)
    causal = positions[:, None] >= positions[None, :]
    strictly = positions[:, None] > positions[None, :]
    identity = jnp.eye(tokens, dtype=jnp.float32)
    normed_in = rms_norm(stream, norm_gain[0]).astype(jnp.bfloat16).reshape(-1, model_width)

    def project(weight):
        result = jnp.dot(normed_in, weight[0], preferred_element_type=jnp.float32)
        return result.reshape(seq_count, tokens, -1)

    query = project(query_weight)
    key = project(key_weight)
    value = project(value_weight)
    zgate = project(zgate_weight)
    gates = jnp.einsum(
        "md,gd->mg", normed_in, gate_weight[0][:, :, 0], preferred_element_type=jnp.float32
    )
    log_decay = (-decay_rate[0, 0] * jax.nn.softplus(gates[:, 0])).reshape(seq_count, tokens)
    strength = jax.nn.sigmoid(gates[:, 1]).reshape(seq_count, tokens)
    values_full = lax.all_gather(value, "rows", axis=2, tiled=True)
    shard_state = recurrent_state[0][:, 0]
    lengths = lax.psum((jnp.sum(query * query, axis=-1), jnp.sum(key * key, axis=-1)), "rows")
    query_scale = lax.rsqrt(lengths[0] + epsilon) * DK ** (-0.5)
    key_scale = lax.rsqrt(lengths[1] + epsilon)
    normalized_query = query * query_scale[..., None]
    normalized_key = key * key_scale[..., None]
    key_lookups = jnp.einsum("bra,bad->brd", normalized_key, shard_state, precision=highest_score)
    query_lookups = jnp.einsum(
        "bra,bad->brd", normalized_query, shard_state, precision=highest_score
    )
    key_gram = jnp.einsum("stk,sjk->stj", normalized_key, normalized_key, precision=highest_score)
    cross_gram = jnp.einsum(
        "stk,sjk->stj", normalized_query, normalized_key, precision=highest_score
    )
    key_lookups, query_lookups, key_gram, cross_gram = (
        lax.psum(key_lookups.astype(jnp.bfloat16), "rows").astype(jnp.float32),
        lax.psum(query_lookups.astype(jnp.bfloat16), "rows").astype(jnp.float32),
        lax.psum(key_gram.astype(jnp.bfloat16), "rows").astype(jnp.float32),
        lax.psum(cross_gram.astype(jnp.bfloat16), "rows").astype(jnp.float32),
    )
    log_gates = jnp.cumsum(log_decay, axis=1)
    spacing = log_gates[:, :, None] - log_gates[:, None, :]
    ratio = jnp.where(causal, jnp.exp(jnp.where(causal, spacing, 0.0)), 0.0)
    lower = jnp.where(strictly, strength[:, :, None] * ratio * key_gram, 0.0)
    right_side = strength[..., None] * (values_full - jnp.exp(log_gates)[..., None] * key_lookups)
    system = identity + lower
    state_updates = lax.linalg.triangular_solve(
        system, right_side, left_side=True, lower=True, unit_diagonal=True
    )
    readouts = jnp.exp(log_gates)[..., None] * query_lookups + jnp.einsum(
        "stj,sjv->stv", ratio * cross_gram, state_updates, precision=highest_score
    )
    leftover_rows = jnp.exp(log_gates[:, -1:] - log_gates)
    new_local = jnp.exp(log_gates[:, -1])[:, None, None] * shard_state + jnp.einsum(
        "gyl,gyx->glx",
        normalized_key,
        leftover_rows[..., None] * state_updates,
        precision=highest_score,
    )
    states_out = [new_local[:, None]]
    columns = value.shape[2]
    row_group = lax.axis_index("rows")
    readout_piece = lax.dynamic_slice_in_dim(readouts, row_group * columns, columns, 2)
    inverse = lax.rsqrt(jnp.mean(readouts * readouts, axis=-1, keepdims=True) + epsilon)
    gated = (readout_piece * inverse * output_gain[0] * jax.nn.silu(zgate)).astype(jnp.bfloat16)
    partial_value = jnp.dot(
        gated.reshape(-1, columns), output_weight[0], preferred_element_type=jnp.float32
    )
    partial_value = partial_value.reshape(seq_count, tokens, model_width)
    stream = stream + layer_total(partial_value)
    final_in = rms_norm(stream, final_gain).astype(jnp.bfloat16)
    gathered = lax.all_gather(final_in, "dp", axis=0, tiled=True)
    logits = jnp.dot(
        gathered.reshape(-1, model_width), vocab_weight, preferred_element_type=jnp.float32
    )
    local_peak = jnp.max(logits, axis=-1)
    local_sum = jnp.sum(jnp.exp(logits - local_peak[:, None]), axis=-1)
    row_peak, row_sum = joined((local_peak, local_sum), ("dp", "rows", "heads"), merge_pair)
    log_total = row_peak + jnp.log(row_sum)
    log_probs = (logits - log_total[:, None]).reshape(gathered.shape[0], tokens, -1)
    return (jnp.stack(states_out), log_probs)


def solution(mesh):
    in_specs = (
        P("dp", None, None),
        P(),
        P(None, None, ("heads", "rows")),
        P(None, None, ("heads", "rows")),
        P(None, None, ("heads", "rows")),
        P(None, None, ("heads", "rows")),
        P(None, None, None, "heads"),
        P(None, "heads"),
        P(None, "rows"),
        P(None, ("heads", "rows"), None),
        P(None, "dp", "heads", "rows", None),
        P(),
        P(None, ("dp", "rows", "heads")),
    )
    out_specs = (P(None, "dp", "heads", "rows", None), P(None, None, ("dp", "rows", "heads")))
    return jax.shard_map(
        on_device, mesh=mesh, in_specs=in_specs, out_specs=out_specs, check_vma=False
    )
```

profile of v0, /device:TPU:0, one launch (start us, length us, event | category | flops | bytes accessed | tf_op | source)
XLA Modules:
  0.0 246.9 jit_solution(2461869967567048000)
XLA Ops:
  7.2 1.0 fusion.19
  8.3 1.7 multiply_reduce_fusion.3
  10.0 1.7 multiply_reduce_fusion.2
  11.7 11.4 %all-reduce.3 = (f32[1,16]{1,0:T(1,128)S(1)}, f32[1,16]{1,0:T(1,128)S(1)}) all-reduce(f32[1,16]{1,0:T(1,128)S(1)} %bitcast.157, f32[1,16]{1,0:T(1,128)S(1)} %bitcast.158), channel_id=1, replica_groups=mesh['dp'=2,'rows'=4,'heads'=4] {'rows'}, use_global_device_ids=true, to_apply=%region_3.4 | all-reduce | flops 32 | bytes 256 | tf_op jit(solution)/shard_map/psum | solution.py:74
  23.1 0.8 fusion.6
  24.7 2.5 fusion.5
  27.1 2.5 fusion.4
  30.3 1.1 fusion.52
  33.6 1.6 fusion.13
  35.1 7.3 %all-gather = f32[16,1024]{1,0:T(8,128)S(1)} all-gather(f32[16,256]{1,0:T(8,128)S(1)} %fusion.13), channel_id=2, replica_groups=mesh['dp'=2,'rows'=4,'heads'=4] {'rows'}, dimensions={1}, use_global_device_ids=true | all-gather | bytes 81920 | tf_op jit(solution)/shard_map/all_gather | solution.py:72
  42.4 27.9 %all-reduce.10.cloned.1.call-done = (bf16[1,16,1024]{2,1,0:T(8,128)(2,1)}, bf16[1,16,16]{2,1,0:T(8,128)(2,1)}, bf16[1,16,1024]{2,1,0:T(8,128)(2,1)}, bf16[1,16,16]{2,1,0:T(8,128)(2,1)}) async-done(((bf16[1,16,1024]{2,1,0:T(8,128)(2,1)}, bf16[1,16,16]{2,1,0:T(8,128)(2,1)}, bf16[1,16,1024]{2,1,0:T(8,128)(2,1)}, bf16[1,16,16]{2,1,0:T(8,128)(2,1)}), (bf16[1,16,1024]{2,1,0:T(8,128)(2,1)}, ...) | async-done | bytes 66576 | tf_op jit(solution)/shard_map/psum | solution.py:88
  71.0 1.2 custom-call.3
  72.3 1.0 fusion.23
  73.3 1.1 multiply_reduce_fusion.1
  74.5 2.7 %convolution_bitcast_fusion = f32[1,16,2048]{2,1,0:T(8,128)} fusion(bf16[1,256,2048]{2,1,0:T(8,128)(2,1)S(1)} %copy-done, bf16[1,2048,256]{2,1,0:T(8,128)(2,1)} %param.20, f32[1,16,1024]{2,1,0:T(8,128)S(1)} %get-tuple-element.164, s32[]{:T(128)S(6)} %select_n.63, f32[256]{0:T(256)} %bitcast.156, f32[16]{0:T(128)S(1)} %add_rsqrt_fusion.1, ...), kind=kOutput, calls=%fused_computation.6 | convolution fusion | flops 33718272 | bytes 2320388 | tf_op jit(solution)/shard_map/dot_general | solution.py:118
  77.2 3.3 %fusion.2 = f32[1,1,1,256,1024]{4,3,2,1,0:T(8,128)} fusion(f32[1,1,1,256,1024]{4,3,2,1,0:T(8,128)} %param.25, f32[]{:T(128)} %bitcast.7, f32[16,1024]{1,0:T(8,128)S(1)} %fusion.23, f32[16]{0:T(128)S(1)} %get-tuple-element.157, f32[16,256]{1,0:T(8,128)S(1)} %get-tuple-element.160, f32[16]{0:T(128)S(1)} %rsqrt_bitcast_fusion), kind=kOutput, calls=%fused_computation.8 | convolution fusion | flops 50876416 | bytes 2179204 | tf_op jit(solution)/shard_map/gyl,gyx->glx/dot_general | solution.py:106
  80.5 104.0 %all-reduce.8.cloned.1.call-done = f32[1,16,2048]{2,1,0:T(8,128)} async-done(((f32[1,16,2048]{2,1,0:T(8,128)}), f32[1,16,2048]{2,1,0:T(8,128)}) %all-reduce.8.cloned.1.call-update) | async-done | bytes 131088 | tf_op jit(solution)/shard_map/psum | solution.py:27
  184.5 1.0 multiply_reduce_fusion
  185.5 1.0 multiply_convert_fusion
  186.6 1.9 all_gather.19
  188.5 8.9 %fusion.82 = (f32[32]{0:T(128)S(1)}, f32[32,4096]{1,0:T(8,128)S(1)}) fusion(bf16[32,2048]{1,0:T(8,128)(2,1)S(1)} %bitcast.147, bf16[2048,4096]{1,0:T(8,128)(2,1)} %param.27), kind=kOutput, calls=%fused_computation.113 | convolution fusion | flops 537001984 | bytes 17432704 | tf_op jit(solution)/shard_map/dot_general | solution.py:125
  198.1 39.5 %all-reduce.2 = (f32[1024]{0:T(1024)S(1)}, f32[1024]{0:T(1024)S(1)}) all-reduce(f32[1024]{0:T(1024)S(1)} %dynamic-update-slice, f32[1024]{0:T(1024)S(1)} %dynamic-update-slice.1), channel_id=3, replica_groups=mesh['dp'=2,'rows'=4,'heads'=4] {'dp','rows','heads'}, use_global_device_ids=true, to_apply=%add | all-reduce | flops 2048 | bytes 16384
  237.8 1.4 while.17
  239.2 0.9 broadcast_subtract_fusion
  (60 shorter events, 4.9 us)
Async XLA Ops:
  7.2 67.3 %copy-start = (bf16[1,256,2048]{2,1,0:T(8,128)(2,1)S(1)}, bf16[1,256,2048]{2,1,0:T(8,128)(2,1)}, u32[]{:S(2)}) copy-start(bf16[1,256,2048]{2,1,0:T(8,128)(2,1)} %param.24) | copy-start | bytes 3145732
  7.2 63.1 %all-reduce.10.cloned.1.call-start = ((), (), s32[]{:S(2)}) async-start(), calls=%async_computation.1 | async-start | bytes 147456 | tf_op jit(solution)/shard_map/psum | solution.py:88
  29.6 154.9 %all-reduce.8.cloned.1.call-start = ((), (), s32[]{:S(2)}) async-start(), calls=%async_computation | async-start | bytes 262144 | tf_op jit(solution)/shard_map/psum | solution.py:27
Sparse Core Ops, SparseCore 0:
  29.7 40.4 all-reduce.9
  77.4 107.0 all-reduce.7
where the time goes:
time: 248 us; the launch traced here: 247 us
  waiting for transfers between devices  132 us (53%)
  blocking collectives  60.1 us (24%)
  matrix products  29.6 us (12%)
  between operations  15.5 us (6%)
  other arithmetic  8.01 us (3%)
    psum x1, waiting for transfers between devices, layer_total(): return lax.psum(partial_value, ('rows', 'heads'))  104 us
    unnamed x1, blocking collectives  39.5 us
    psum x1, waiting for transfers between devices, on_device(): lax.psum(key_lookups.astype(jnp.bfloat16), 'rows').astype(jnp.float32)  27.9 us
    psum x1, blocking collectives, on_device(): lax.psum((jnp.sum(query * query, axis=-1), jnp.sum(key * key, axis=-1)),...  11.4 us
    dot_general x1, matrix products, on_device(): jnp.dot(gathered.reshape(-1, model_width), vocab_weight, preferred_elemen...  8.86 us
    all_gather x1, blocking collectives, on_device(): values_full = lax.all_gather(value, 'rows', axis=2, tiled=True)  7.27 us
  transfers between devices with their start and end apart: 2, of which 2 were waited for; matrix products, arithmetic and copies ran while one was open for 3% of the time, Pallas kernels for 0%

commit v1 on v0

v1 whole, which is shorter than its diff:
```python
import functools

import jax
import jax.numpy as jnp
from jax import lax
from jax.experimental import pallas as pl
from jax.experimental.pallas import tpu as pltpu
from jax.sharding import PartitionSpec as P

MESH = pl.DeviceIdType.MESH
f32 = jnp.float32
bf16 = jnp.bfloat16
epsilon = 1e-06
HIGHEST = lax.Precision.HIGHEST
LANES = 128


def halves(x):
    high = x.astype(bf16)
    return high, (x - high.astype(f32)).astype(bf16)


def dot(a, b, dims=((1,), (0,)), precision=None):
    return lax.dot_general(a, b, (dims, ((), ())), precision=precision, preferred_element_type=f32)


def exchange(n, me, src_of, dst, send, recv, device_of):
    def other(k):
        return lax.rem(me + k, n)

    def outgoing(p):
        return pltpu.make_async_remote_copy(
            src_ref=src_of(p), dst_ref=dst.at[me], send_sem=send.at[p], recv_sem=recv.at[me],
            device_id=device_of(p), device_id_type=MESH)

    def incoming(p):
        return pltpu.make_async_remote_copy(
            src_ref=dst.at[p], dst_ref=dst.at[p], send_sem=send.at[p], recv_sem=recv.at[p],
            device_id=device_of(p), device_id_type=MESH)

    def over(act):
        def step(k, _):
            act(other(k))
            return 0

        lax.fori_loop(1, n, step, 0)

    over(lambda p: outgoing(p).start())
    return (lambda: over(lambda p: incoming(p).wait_recv()),
            lambda: over(lambda p: outgoing(p).wait_send()))


def kernel(shape, chunks,
           hidden, norm_gain, qw, kw, vw, zw, gw, rate, ogain, ow, state, fgain, vocab,
           new_state, logits_out, total_out,
           hid_v, ngain_v, qw_v, kw_v, vw_v, zw_v, gw_v, rate_v, ogain_v, ow_v, state_v, fgain_v, voc_v,
           aux, look, read_v, parts, rs, ag, fin, stats, ns_v, log_v, tot_v,
           in_sem, voc_sem, out_sem,
           aux_s, aux_r, look_s, look_r, rs_s, rs_r, ag_s, ag_r, fin_s, fin_r, st_s, st_r):
    dps, rows, heads = shape["dp"], shape["rows"], shape["heads"]
    group = rows * heads
    everyone = dps * group
    d, r, h = (lax.axis_index(a) for a in ("dp", "rows", "heads"))
    g = r * heads + h
    me = d * group + g
    tokens, width = hid_v.shape
    vs = vw_v.shape[1]

    def in_group(p):
        return {"dp": d, "rows": lax.div(p, heads), "heads": lax.rem(p, heads)}

    def anywhere(p):
        q = lax.rem(p, group)
        return {"dp": lax.div(p, group), "rows": lax.div(q, heads), "heads": lax.rem(q, heads)}

    def in_rows(p):
        return {"dp": d, "rows": p, "heads": h}

    def in_dp(p):
        return {"dp": p, "rows": r, "heads": h}

    loads = {}
    order = (("hid", hidden, hid_v), ("ngain", norm_gain, ngain_v), ("kw", kw, kw_v), ("qw", qw, qw_v),
             ("vw", vw, vw_v), ("state", state, state_v), ("gw", gw, gw_v), ("rate", rate, rate_v),
             ("zw", zw, zw_v), ("ogain", ogain, ogain_v), ("fgain", fgain, fgain_v), ("ow", ow, ow_v))
    for i, (name, src, dst) in enumerate(order):
        loads[name] = pltpu.make_async_copy(src, dst, in_sem.at[i])
        loads[name].start()
    barrier = pltpu.get_barrier_semaphore()

    def greet(k, _):
        pl.semaphore_signal(barrier, inc=1, device_id=anywhere(lax.rem(me + k, everyone)), device_id_type=MESH)
        return 0

    lax.fori_loop(1, everyone, greet, 0)

    loads["hid"].wait()
    loads["ngain"].wait()
    stream = hid_v[...].astype(f32)
    normed = (stream * lax.rsqrt(jnp.mean(stream * stream, axis=-1, keepdims=True) + epsilon) * ngain_v[...]).astype(bf16)
    loads["kw"].wait()
    key = dot(normed, kw_v[...])
    loads["qw"].wait()
    query = dot(normed, qw_v[...])
    loads["vw"].wait()
    value = dot(normed, vw_v[...])

    both = jnp.concatenate([query, key], axis=0)
    wide = jnp.concatenate([key, query, jnp.zeros((LANES - 2 * tokens, key.shape[1]), f32)], axis=0)
    grams = dot(both, wide, ((1,), (1,)), HIGHEST)
    aux[r, :, pl.ds(0, vs)] = value
    aux[r, :, pl.ds(vs, LANES)] = grams[:tokens]
    aux[r, :, pl.ds(vs + LANES, LANES)] = grams[tokens:]
    pl.semaphore_wait(barrier, everyone - 1)
    aux_wait, aux_end = exchange(rows, r, lambda p: aux.at[r], aux, aux_s, aux_r, in_rows)

    loads["state"].wait()
    s_high, s_low = halves(state_v[...])
    b_high, b_low = halves(both)
    first = dot(jnp.concatenate([b_high, b_low], axis=0), s_high)
    found = first[:2 * tokens] + first[2 * tokens:] + dot(b_high, s_low)
    look[r] = found.astype(bf16)
    look_wait, look_end = exchange(rows, r, lambda p: look.at[r], look, look_s, look_r, in_rows)

    cw = voc_v.shape[1] // chunks
    vloads = []
    for c in range(chunks):
        at = pl.ds(c * cw, cw)
        vloads.append(pltpu.make_async_copy(vocab.at[:, at], voc_v.at[:, at], voc_sem.at[c]))
        vloads[-1].start()

    loads["gw"].wait()
    loads["rate"].wait()
    normed32 = normed.astype(f32)
    gate0 = jnp.sum(normed32 * gw_v[0:1, :].astype(f32), axis=1, keepdims=True)
    gate1 = jnp.sum(normed32 * gw_v[1:2, :].astype(f32), axis=1, keepdims=True)
    softplus = jnp.maximum(gate0, 0.0) + jnp.log1p(jnp.exp(-jnp.abs(gate0)))
    log_decay = -rate_v[...] * softplus
    strength = jax.nn.sigmoid(gate1)
    row = lax.broadcasted_iota(jnp.int32, (tokens, LANES), 0)
    col = lax.broadcasted_iota(jnp.int32, (tokens, LANES), 1)
    same = row == col
    causal = row >= col
    strictly = row > col

    def as_row(column):
        return jnp.sum(jnp.where(same, column, 0.0), axis=0, keepdims=True)

    reach = jnp.sum(jnp.where(causal, as_row(log_decay), 0.0), axis=1, keepdims=True)
    reach_row = as_row(reach)
    ratio = jnp.where(causal, jnp.exp(jnp.where(causal, reach - reach_row, 0.0)), 0.0)
    decay = jnp.exp(reach)
    last = reach[tokens - 1:tokens, :]
    loads["zw"].wait()
    zgate = dot(normed, zw_v[...])
    silu = zgate * jax.nn.sigmoid(zgate)

    aux_wait()
    gq = aux[0, :, pl.ds(vs, LANES)]
    gk = aux[0, :, pl.ds(vs + LANES, LANES)]
    for p in range(1, rows):
        gq += aux[p, :, pl.ds(vs, LANES)]
        gk += aux[p, :, pl.ds(vs + LANES, LANES)]
    values = jnp.concatenate([aux[p, :, pl.ds(0, vs)] for p in range(rows)], axis=1)
    dk = shape["dk"]
    k_len = jnp.sum(jnp.where(same, gk, 0.0), axis=1, keepdims=True)
    q_len = jnp.sum(jnp.where(col == row + tokens, gq, 0.0), axis=1, keepdims=True)
    k_scale = lax.rsqrt(k_len + epsilon)
    q_scale = lax.rsqrt(q_len + epsilon) * dk ** (-0.5)
    k_scale_row = as_row(k_scale)
    lower = jnp.where(strictly, strength * ratio * (gk * k_scale * k_scale_row), 0.0)
    cross = ratio * (gq * q_scale * k_scale_row)
    inverse = jnp.where(same, 1.0, 0.0)
    for i in range(tokens - 1):
        inverse = inverse - lower[:, i:i + 1] * inverse[i:i + 1, :]
    inverse = inverse[:, :tokens]
    reader = dot(cross[:, :tokens], inverse, precision=HIGHEST)
    solver = jnp.concatenate([inverse, reader], axis=0)

    look_wait()
    looked = look[0].astype(f32)
    for p in range(1, rows):
        looked += look[p].astype(f32)
    right = strength * (values - decay * k_scale * looked[tokens:])
    solved = dot(solver, right, precision=HIGHEST)
    updates = solved[:tokens]
    readouts = decay * q_scale * looked[:tokens] + solved[tokens:]
    read_v[...] = readouts
    norm = lax.rsqrt(jnp.mean(readouts * readouts, axis=-1, keepdims=True) + epsilon)
    piece = read_v[:, pl.ds(pl.multiple_of(r * vs, LANES), vs)]
    loads["ogain"].wait()
    gated = (piece * norm * ogain_v[...] * silu).astype(bf16)
    loads["ow"].wait()
    partial = dot(gated, ow_v[...])
    cut = width // group
    for p in range(group):
        parts[p] = partial[:, p * cut:(p + 1) * cut].astype(parts.dtype)
    rs_wait, rs_end = exchange(group, g, lambda p: parts.at[p], rs, rs_s, rs_r, in_group)
    rs[g] = parts[g]

    u_high, u_low = halves(jnp.exp(last - reach) * updates)
    k_high, k_low = halves(key * k_scale)
    ins = ((0,), (0,))
    grown = dot(k_high, u_high, ins) + dot(k_high, u_low, ins) + dot(k_low, u_high, ins)
    ns_v[...] = jnp.exp(last) * state_v[...] + grown
    ns_store = pltpu.make_async_copy(ns_v, new_state, out_sem.at[0])
    ns_store.start()

    rs_wait()
    mixed = rs[0].astype(f32)
    for p in range(1, group):
        mixed += rs[p].astype(f32)
    ag[g] = mixed.astype(ag.dtype)
    ag_wait, ag_end = exchange(group, g, lambda p: ag.at[g], ag, ag_s, ag_r, in_group)
    loads["fgain"].wait()
    ag_wait()
    stream = hid_v[...].astype(f32) + jnp.concatenate([ag[p].astype(f32) for p in range(group)], axis=1)
    fin[d] = (stream * lax.rsqrt(jnp.mean(stream * stream, axis=-1, keepdims=True) + epsilon) * fgain_v[...]).astype(bf16)
    fin_wait, fin_end = exchange(dps, d, lambda p: fin.at[d], fin, fin_s, fin_r, in_dp)
    fin_wait()
    final = fin[...].reshape(dps * tokens, width)
    for c in range(chunks):
        at = pl.ds(c * cw, cw)
        vloads[c].wait()
        log_v[:, at] = dot(final, voc_v[:, at])
    logits_store = pltpu.make_async_copy(log_v, logits_out, out_sem.at[1])
    logits_store.start()
    logits = log_v[...]
    peak = jnp.max(logits, axis=1, keepdims=True)
    total = jnp.sum(jnp.exp(logits - peak), axis=1, keepdims=True)
    scored, lanes = dps * tokens, stats.shape[2]
    diagonal = (lax.broadcasted_iota(jnp.int32, (scored, lanes), 0)
                == lax.broadcasted_iota(jnp.int32, (scored, lanes), 1))
    stats[me, 0:1, :] = jnp.sum(jnp.where(diagonal, peak, 0.0), axis=0, keepdims=True)
    stats[me, 1:2, :] = jnp.sum(jnp.where(diagonal, total, 0.0), axis=0, keepdims=True)
    st_wait, st_end = exchange(everyone, me, lambda p: stats.at[me], stats, st_s, st_r, anywhere)
    for end in (aux_end, look_end, rs_end, ag_end, fin_end):
        end()
    ns_store.wait()
    logits_store.wait()
    st_wait()
    peaks = stats[:, 0, :]
    sums = stats[:, 1, :]
    top = jnp.max(peaks, axis=0, keepdims=True)
    log_total = top + jnp.log(jnp.sum(sums * jnp.exp(peaks - top), axis=0, keepdims=True))
    tot_v[...] = jnp.broadcast_to(
        jnp.sum(jnp.where(diagonal, log_total, 0.0), axis=1, keepdims=True), tot_v.shape)
    tot_store = pltpu.make_async_copy(tot_v, total_out, out_sem.at[2])
    tot_store.start()
    st_end()
    tot_store.wait()


def on_device(shape, hidden, norm_gain, qw, kw, vw, zw, gw, rate, ogain, ow, state, fgain, vocab):
    seqs, tokens, width = hidden.shape
    assert seqs == 1 and hidden.shape[0] == state.shape[1] and norm_gain.shape[0] == 1
    dps, rows, heads = shape["dp"], shape["rows"], shape["heads"]
    group, everyone = rows * heads, dps * rows * heads
    ks, dv = state.shape[3:]
    vs, vl = vw.shape[2], vocab.shape[1]
    scored = dps * tokens
    lanes = -(-scored // LANES) * LANES
    chunks = max(1, vl // 512)
    shape = dict(shape, dk=ks * rows)
    args = (hidden[0], norm_gain, qw[0], kw[0], vw[0], zw[0], gw[0, :, :, 0], rate, ogain, ow[0],
            state[0, 0, 0], fgain.reshape(1, -1), vocab)
    dma = pltpu.SemaphoreType.DMA
    scratch = [pltpu.VMEM(a.shape, a.dtype) for a in args] + [
        pltpu.VMEM((rows, tokens, vs + 2 * LANES), f32),
        pltpu.VMEM((rows, 2 * tokens, dv), bf16),
        pltpu.VMEM((tokens, dv), f32),
        pltpu.VMEM((group, tokens, width // group), bf16),
        pltpu.VMEM((group, tokens, width // group), bf16),
        pltpu.VMEM((group, tokens, width // group), bf16),
        pltpu.VMEM((dps, tokens, width), bf16),
        pltpu.VMEM((everyone, 2, lanes), f32),
        pltpu.VMEM((ks, dv), f32),
        pltpu.VMEM((scored, vl), f32),
        pltpu.VMEM((scored, LANES), f32),
        dma((12,)), dma((chunks,)), dma((3,)),
    ] + [dma((n,)) for n in (rows, rows, rows, rows, group, group, group, group, dps, dps, everyone, everyone)]
    anywhere = pl.BlockSpec(memory_space=pl.ANY)
    new_state, logits, total = pl.pallas_call(
        functools.partial(kernel, shape, chunks),
        out_shape=(jax.ShapeDtypeStruct((ks, dv), f32), jax.ShapeDtypeStruct((scored, vl), f32),
                   jax.ShapeDtypeStruct((scored, LANES), f32)),
        in_specs=[anywhere] * len(args),
        out_specs=(anywhere,) * 3,
        scratch_shapes=scratch,
        compiler_params=pltpu.CompilerParams(
            collective_id=0, has_side_effects=True, vmem_limit_bytes=48 * 1024 * 1024),
    )(*args)
    log_probs = (logits - total[:, :1]).reshape(dps, tokens, vl)
    return new_state.reshape(state.shape), log_probs


def solution(mesh):
    in_specs = (
        P("dp", None, None),
        P(),
        P(None, None, ("heads", "rows")),
        P(None, None, ("heads", "rows")),
        P(None, None, ("heads", "rows")),
        P(None, None, ("heads", "rows")),
        P(None, None, None, "heads"),
        P(None, "heads"),
        P(None, "rows"),
        P(None, ("heads", "rows"), None),
        P(None, "dp", "heads", "rows", None),
        P(),
        P(None, ("dp", "rows", "heads")),
    )
    out_specs = (P(None, "dp", "heads", "rows", None), P(None, None, ("dp", "rows", "heads")))
    return jax.shard_map(functools.partial(on_device, dict(mesh.shape)), mesh=mesh, in_specs=in_specs,
                         out_specs=out_specs, check_vma=False)
```

time: 248 us -> 46.2 us (0.19)
  waiting for transfers between devices: 132 us -> 0 us
  blocking collectives: 60.1 us -> 0 us
  Pallas kernels: 0 us -> 34 us
  matrix products: 29.6 us -> 0 us
  between operations: 15.5 us -> 1.31 us
  local copies, waits for them, and re-layouts: 1.26 us -> 9.58 us
  other arithmetic: 8.01 us -> 0.91 us
    psum x2 -> x0, waiting for transfers between devices: 132 us -> none  [the longest x1 104 us: layer_total(): return lax.psum(partial_value, ('rows', 'heads'))]
    unnamed x1 -> x0, blocking collectives: 39.5 us -> none
    pallas_call x0 -> x1, Pallas kernels: none -> 34 us  [on_device(): pl.pallas_call(functools.partial(kernel, shape, chunks), out_shape=(jax.S...]
    dot_general x12 -> x0, matrix products: 28.6 us -> none  [the longest x1 8.86 us: on_device(): jnp.dot(gathered.reshape(-1, model_width), vocab_weight, preferred_elemen...]
    psum x1 -> x0, blocking collectives: 11.4 us -> none  [on_device(): lax.psum((jnp.sum(query * query, axis=-1), jnp.sum(key * key, axis=-1)),...]
    all_gather x2 -> x0, blocking collectives: 9.17 us -> none  [the longest x1 7.27 us: on_device(): values_full = lax.all_gather(value, 'rows', axis=2, tiled=True)]
    unnamed x6 -> x19, local copies, waits for them, and re-layouts: 0.47 us -> 9.47 us
  transfers between devices with their start and end apart: 2 -> 0, of which waited for: 2 -> 0; matrix products, arithmetic and copies ran while one was open for 3% -> 0% of each run, Pallas kernels for 0% -> 0%
where the time goes in v1:
time: 46.2 us; the launch traced here: 45.8 us
  Pallas kernels  34 us (74%)
  local copies, waits for them, and re-layouts  9.58 us (21%)
  between operations  1.31 us (3%)
  other arithmetic  0.91 us (2%)
    pallas_call x1, Pallas kernels, on_device(): pl.pallas_call(functools.partial(kernel, shape, chunks), out_shape=(jax.S...  34 us
    unnamed x19, local copies, waits for them, and re-layouts  9.47 us

profile of v1, /device:TPU:0, one launch (start us, length us, event | category | flops | bytes accessed | tf_op | source)
XLA Modules:
  0.0 45.8 jit_solution(17665916836048944584)
XLA Ops:
  1.3 0.0 copy-start
  1.3 1.2 %copy-done = bf16[1,2048,256]{2,1,0:T(8,128)(2,1)S(1)} copy-done((bf16[1,2048,256]{2,1,0:T(8,128)(2,1)S(1)}, bf16[1,2048,256]{2,1,0:T(8,128)(2,1)}, u32[]{:S(2)}) %copy-start) | copy-done | bytes 1048600
  2.5 0.0 copy-start.1
  2.5 1.2 %copy-done.1 = bf16[1,2048,256]{2,1,0:T(8,128)(2,1)S(1)} copy-done((bf16[1,2048,256]{2,1,0:T(8,128)(2,1)S(1)}, bf16[1,2048,256]{2,1,0:T(8,128)(2,1)}, u32[]{:S(2)}) %copy-start.1) | copy-done | bytes 1048600
  3.7 0.0 copy-start.2
  3.7 1.2 %copy-done.2 = bf16[1,2048,256]{2,1,0:T(8,128)(2,1)S(1)} copy-done((bf16[1,2048,256]{2,1,0:T(8,128)(2,1)S(1)}, bf16[1,2048,256]{2,1,0:T(8,128)(2,1)}, u32[]{:S(2)}) %copy-start.2) | copy-done | bytes 1048600
  5.0 0.0 copy-start.3
  5.0 1.2 %copy-done.3 = bf16[1,2048,256]{2,1,0:T(8,128)(2,1)S(1)} copy-done((bf16[1,2048,256]{2,1,0:T(8,128)(2,1)S(1)}, bf16[1,2048,256]{2,1,0:T(8,128)(2,1)}, u32[]{:S(2)}) %copy-start.3) | copy-done | bytes 1048600
  6.2 0.0 copy-start.4
  6.2 0.8 %copy-done.4 = bf16[1,16,2048]{2,1,0:T(8,128)(2,1)S(1)} copy-done((bf16[1,16,2048]{2,1,0:T(8,128)(2,1)S(1)}, bf16[1,16,2048]{2,1,0:T(8,128)(2,1)}, u32[]{:S(2)}) %copy-start.4) | copy-done | bytes 65560
  7.0 0.0 copy-start.5
  7.0 0.7 %copy-done.5 = f32[1,2048]{1,0:T(1,128)S(1)} copy-done((f32[1,2048]{1,0:T(1,128)S(1)}, f32[1,2048]{1,0:T(1,128)}, u32[]{:S(2)}) %copy-start.5) | copy-done | bytes 8216
  7.7 0.0 copy-start.6
  7.7 0.7 %copy-done.6 = bf16[1,2,2048,1]{2,1,3,0:T(2,128)(2,1)S(1)} copy-done((bf16[1,2,2048,1]{2,1,3,0:T(2,128)(2,1)S(1)}, bf16[1,2,2048,1]{2,1,3,0:T(2,128)(2,1)}, u32[]{:S(2)}) %copy-start.6) | copy-done | bytes 8216
  8.4 0.0 copy-start.7
  8.4 0.7 %copy-done.7 = f32[2048]{0:T(1024)S(1)} copy-done((f32[2048]{0:T(1024)S(1)}, f32[2048]{0:T(1024)}, u32[]{:S(2)}) %copy-start.7) | copy-done | bytes 8216
  9.1 0.0 copy-start.8
  9.1 0.7 %copy-done.8 = f32[1,256]{1,0:T(1,128)S(1)} copy-done((f32[1,256]{1,0:T(1,128)S(1)}, f32[1,256]{1,0:T(1,128)}, u32[]{:S(2)}) %copy-start.8) | copy-done | bytes 1048
  9.8 34.0 %shard_map.140 = (f32[256,1024]{1,0:T(8,128)S(1)}, f32[32,4096]{1,0:T(8,128)S(1)}, f32[32,128]{1,0:T(8,128)S(1)}) custom-call(bf16[16,2048]{1,0:T(8,128)(2,1)S(1)} %bitcast.16, f32[1,2048]{1,0:T(1,128)S(1)} %copy-done.5, bf16[2048,256]{1,0:T(8,128)(2,1)S(1)} %bitcast.11, bf16[2048,256]{1,0:T(8,128)(2,1)S(1)} %bitcast.12, bf16[2048,256]{1,0:T(8,128)(2,1)S(1)} %bitcast.13, ...), custom_call_target="tpu_custom_call" | custom-call | tf_op jit(solution)/shard_map/pallas_call | solution.py:283
  43.8 0.1 slice_reduce_fusion
  43.9 0.9 %broadcast_subtract_fusion = f32[32,4096]{1,0:T(8,128)} fusion(f32[32,4096]{1,0:T(8,128)S(1)} %get-tuple-element.6, f32[32]{0:T(128)S(1)} %slice_reduce_fusion), kind=kLoop, calls=%fused_computation | loop fusion | flops 131072 | bytes 1048704 | tf_op jit(solution)/shard_map/sub | solution.py:293
  44.8 1.0 %copy.17 = f32[1,1,1,256,1024]{4,3,2,1,0:T(8,128)} copy(f32[1,1,1,256,1024]{4,3,2,1,0:T(8,128)S(1)} %bitcast.15) | data formatting | bytes 2097152
Async XLA Ops:
  1.3 1.2 %copy-start = (bf16[1,2048,256]{2,1,0:T(8,128)(2,1)S(1)}, bf16[1,2048,256]{2,1,0:T(8,128)(2,1)}, u32[]{:S(2)}) copy-start(bf16[1,2048,256]{2,1,0:T(8,128)(2,1)} %param.15) | copy-start | bytes 3145732
  2.5 1.2 %copy-start.1 = (bf16[1,2048,256]{2,1,0:T(8,128)(2,1)S(1)}, bf16[1,2048,256]{2,1,0:T(8,128)(2,1)}, u32[]{:S(2)}) copy-start(bf16[1,2048,256]{2,1,0:T(8,128)(2,1)} %param.16) | copy-start | bytes 3145732
  3.7 1.2 %copy-start.2 = (bf16[1,2048,256]{2,1,0:T(8,128)(2,1)S(1)}, bf16[1,2048,256]{2,1,0:T(8,128)(2,1)}, u32[]{:S(2)}) copy-start(bf16[1,2048,256]{2,1,0:T(8,128)(2,1)} %param.17) | copy-start | bytes 3145732
  5.0 1.2 %copy-start.3 = (bf16[1,2048,256]{2,1,0:T(8,128)(2,1)S(1)}, bf16[1,2048,256]{2,1,0:T(8,128)(2,1)}, u32[]{:S(2)}) copy-start(bf16[1,2048,256]{2,1,0:T(8,128)(2,1)} %param.18) | copy-start | bytes 3145732
  6.2 0.8 %copy-start.4 = (bf16[1,16,2048]{2,1,0:T(8,128)(2,1)S(1)}, bf16[1,16,2048]{2,1,0:T(8,128)(2,1)}, u32[]{:S(2)}) copy-start(bf16[1,16,2048]{2,1,0:T(8,128)(2,1)} %param.13) | copy-start | bytes 196612
  7.0 0.7 %copy-start.5 = (f32[1,2048]{1,0:T(1,128)S(1)}, f32[1,2048]{1,0:T(1,128)}, u32[]{:S(2)}) copy-start(f32[1,2048]{1,0:T(1,128)} %norm_gain.1) | copy-start | bytes 24580
  7.7 0.7 %copy-start.6 = (bf16[1,2,2048,1]{2,1,3,0:T(2,128)(2,1)S(1)}, bf16[1,2,2048,1]{2,1,3,0:T(2,128)(2,1)}, u32[]{:S(2)}) copy-start(bf16[1,2,2048,1]{2,1,3,0:T(2,128)(2,1)} %param.19) | copy-start | bytes 24580
  8.4 0.7 %copy-start.7 = (f32[2048]{0:T(1024)S(1)}, f32[2048]{0:T(1024)}, u32[]{:S(2)}) copy-start(f32[2048]{0:T(1024)} %param.24) | copy-start | bytes 24580
  9.1 0.7 %copy-start.8 = (f32[1,256]{1,0:T(1,128)S(1)}, f32[1,256]{1,0:T(1,128)}, u32[]{:S(2)}) copy-start(f32[1,256]{1,0:T(1,128)} %ogain.1) | copy-start | bytes 3076

commit v2 on v1

--- a/solution.py
+++ b/solution.py
@@ -13,6 +13,7 @@
 epsilon = 1e-06
 HIGHEST = lax.Precision.HIGHEST
 LANES = 128
+LIMIT = 62 * 1024 * 1024
 
 
 def halves(x):
@@ -24,9 +25,21 @@
     return lax.dot_general(a, b, (dims, ((), ())), precision=precision, preferred_element_type=f32)
 
 
+def looped(n, step):
+    if n > 64:
+        lax.fori_loop(1, n, step, 0)
+    else:
+        for k in range(1, n):
+            step(k, 0)
+
+
+def wrapped(a, n):
+    return jnp.where(a >= n, a - n, a)
+
+
 def exchange(n, me, src_of, dst, send, recv, device_of):
     def other(k):
-        return lax.rem(me + k, n)
+        return wrapped(me + k, n)
 
     def outgoing(p):
         return pltpu.make_async_remote_copy(
@@ -43,7 +56,7 @@
             act(other(k))
             return 0
 
-        lax.fori_loop(1, n, step, 0)
+        looped(n, step)
 
     over(lambda p: outgoing(p).start())
     return (lambda: over(lambda p: incoming(p).wait_recv()),
@@ -89,10 +102,10 @@
     barrier = pltpu.get_barrier_semaphore()
 
     def greet(k, _):
-        pl.semaphore_signal(barrier, inc=1, device_id=anywhere(lax.rem(me + k, everyone)), device_id_type=MESH)
+        pl.semaphore_signal(barrier, inc=1, device_id=anywhere(wrapped(me + k, everyone)), device_id_type=MESH)
         return 0
 
-    lax.fori_loop(1, everyone, greet, 0)
+    looped(everyone, greet)
 
     loads["hid"].wait()
     loads["ngain"].wait()
@@ -106,11 +119,13 @@
     value = dot(normed, vw_v[...])
 
     both = jnp.concatenate([query, key], axis=0)
-    wide = jnp.concatenate([key, query, jnp.zeros((LANES - 2 * tokens, key.shape[1]), f32)], axis=0)
-    grams = dot(both, wide, ((1,), (1,)), HIGHEST)
+    rest = jnp.zeros((LANES - 3 * tokens, key.shape[1]), f32)
+    none = jnp.zeros_like(key)
+    lanes_in = ((1,), (1,))
+    grams = (dot(key, jnp.concatenate([key, none, none, rest], axis=0), lanes_in, HIGHEST)
+             + dot(query, jnp.concatenate([none, key, query, rest], axis=0), lanes_in, HIGHEST))
     aux[r, :, pl.ds(0, vs)] = value
-    aux[r, :, pl.ds(vs, LANES)] = grams[:tokens]
-    aux[r, :, pl.ds(vs + LANES, LANES)] = grams[tokens:]
+    aux[r, :, pl.ds(vs, LANES)] = grams
     pl.semaphore_wait(barrier, everyone - 1)
     aux_wait, aux_end = exchange(rows, r, lambda p: aux.at[r], aux, aux_s, aux_r, in_rows)
 
@@ -156,25 +171,23 @@
     silu = zgate * jax.nn.sigmoid(zgate)
 
     aux_wait()
-    gq = aux[0, :, pl.ds(vs, LANES)]
-    gk = aux[0, :, pl.ds(vs + LANES, LANES)]
+    gk = aux[0, :, pl.ds(vs, LANES)]
     for p in range(1, rows):
-        gq += aux[p, :, pl.ds(vs, LANES)]
-        gk += aux[p, :, pl.ds(vs + LANES, LANES)]
+        gk += aux[p, :, pl.ds(vs, LANES)]
     values = jnp.concatenate([aux[p, :, pl.ds(0, vs)] for p in range(rows)], axis=1)
     dk = shape["dk"]
     k_len = jnp.sum(jnp.where(same, gk, 0.0), axis=1, keepdims=True)
-    q_len = jnp.sum(jnp.where(col == row + tokens, gq, 0.0), axis=1, keepdims=True)
+    q_len = jnp.sum(jnp.where(col == row + 2 * tokens, gk, 0.0), axis=1, keepdims=True)
     k_scale = lax.rsqrt(k_len + epsilon)
     q_scale = lax.rsqrt(q_len + epsilon) * dk ** (-0.5)
     k_scale_row = as_row(k_scale)
     lower = jnp.where(strictly, strength * ratio * (gk * k_scale * k_scale_row), 0.0)
-    cross = ratio * (gq * q_scale * k_scale_row)
+    cross = ratio[:, :tokens] * (gk[:, tokens:2 * tokens] * q_scale * k_scale_row[:, :tokens])
     inverse = jnp.where(same, 1.0, 0.0)
     for i in range(tokens - 1):
         inverse = inverse - lower[:, i:i + 1] * inverse[i:i + 1, :]
     inverse = inverse[:, :tokens]
-    reader = dot(cross[:, :tokens], inverse, precision=HIGHEST)
+    reader = dot(cross, inverse, precision=HIGHEST)
     solver = jnp.concatenate([inverse, reader], axis=0)
 
     look_wait()
@@ -251,6 +264,33 @@
     tot_store.wait()
 
 
+def finish(state_in, logits_in, total_in, state_out, log_probs_out, state, logits, total, sem_in, sem_out):
+    pieces = sem_in.shape[0] - 2
+    depth = state.shape[0] // pieces
+    half = logits.shape[1] // 2
+    loads = [pltpu.make_async_copy(logits_in, logits, sem_in.at[pieces]),
+             pltpu.make_async_copy(total_in, total, sem_in.at[pieces + 1])]
+    stores = []
+    for i in range(pieces):
+        at = pl.ds(i * depth, depth)
+        loads.append(pltpu.make_async_copy(state_in.at[at], state.at[at], sem_in.at[i]))
+        stores.append(pltpu.make_async_copy(state.at[at], state_out.at[at], sem_out.at[i]))
+    for copy in loads:
+        copy.start()
+    loads[0].wait()
+    loads[1].wait()
+    for i in range(2):
+        at = pl.ds(i * half, half)
+        logits[:, at] = logits[:, at] - total[:, 0:1]
+        stores.append(pltpu.make_async_copy(logits.at[:, at], log_probs_out.at[:, at], sem_out.at[pieces + i]))
+        stores[-1].start()
+    for i in range(pieces):
+        loads[2 + i].wait()
+        stores[i].start()
+    for store in stores:
+        store.wait()
+
+
 def on_device(shape, hidden, norm_gain, qw, kw, vw, zw, gw, rate, ogain, ow, state, fgain, vocab):
     seqs, tokens, width = hidden.shape
     assert seqs == 1 and hidden.shape[0] == state.shape[1] and norm_gain.shape[0] == 1
@@ -266,7 +306,7 @@
             state[0, 0, 0], fgain.reshape(1, -1), vocab)
     dma = pltpu.SemaphoreType.DMA
     scratch = [pltpu.VMEM(a.shape, a.dtype) for a in args] + [
-        pltpu.VMEM((rows, tokens, vs + 2 * LANES), f32),
+        pltpu.VMEM((rows, tokens, vs + LANES), f32),
         pltpu.VMEM((rows, 2 * tokens, dv), bf16),
         pltpu.VMEM((tokens, dv), f32),
         pltpu.VMEM((group, tokens, width // group), bf16),
@@ -279,19 +319,28 @@
         pltpu.VMEM((scored, LANES), f32),
         dma((12,)), dma((chunks,)), dma((3,)),
     ] + [dma((n,)) for n in (rows, rows, rows, rows, group, group, group, group, dps, dps, everyone, everyone)]
-    anywhere = pl.BlockSpec(memory_space=pl.ANY)
-    new_state, logits, total = pl.pallas_call(
+    in_hbm = pl.BlockSpec(memory_space=pltpu.HBM)
+    anyplace = pl.BlockSpec(memory_space=pl.ANY)
+    results = pl.pallas_call(
         functools.partial(kernel, shape, chunks),
         out_shape=(jax.ShapeDtypeStruct((ks, dv), f32), jax.ShapeDtypeStruct((scored, vl), f32),
                    jax.ShapeDtypeStruct((scored, LANES), f32)),
-        in_specs=[anywhere] * len(args),
-        out_specs=(anywhere,) * 3,
+        in_specs=[in_hbm] * len(args),
+        out_specs=(anyplace,) * 3,
         scratch_shapes=scratch,
         compiler_params=pltpu.CompilerParams(
-            collective_id=0, has_side_effects=True, vmem_limit_bytes=48 * 1024 * 1024),
+            collective_id=0, has_side_effects=True, vmem_limit_bytes=LIMIT),
     )(*args)
-    log_probs = (logits - total[:, :1]).reshape(dps, tokens, vl)
-    return new_state.reshape(state.shape), log_probs
+    new_state, log_probs = pl.pallas_call(
+        finish,
+        out_shape=(jax.ShapeDtypeStruct((ks, dv), f32), jax.ShapeDtypeStruct((scored, vl), f32)),
+        in_specs=[anyplace] * 3,
+        out_specs=(anyplace,) * 2,
+        scratch_shapes=[pltpu.VMEM((ks, dv), f32), pltpu.VMEM((scored, vl), f32),
+                        pltpu.VMEM((scored, LANES), f32), dma((6,)), dma((6,))],
+        compiler_params=pltpu.CompilerParams(vmem_limit_bytes=LIMIT),
+    )(*results)
+    return new_state.reshape(state.shape), log_probs.reshape(dps, tokens, vl)
 
 
 def solution(mesh):

time: 46.2 us -> 37.4 us (0.81)
  local copies, waits for them, and re-layouts: 9.58 us -> 0 us
  Pallas kernels: 34 us -> 35.9 us
  other arithmetic: 0.91 us -> 0 us
    unnamed x19 -> x0, local copies, waits for them, and re-layouts: 9.47 us -> none
    pallas_call x0 -> x1, Pallas kernels: none -> 2.37 us  [on_device(): pl.pallas_call(finish, out_shape=(jax.ShapeDtypeStruct((ks, dv), f32), ja...]
    sub x1 -> x0, other arithmetic: 0.91 us -> none  [on_device(): log_probs = (logits - total[:, :1]).reshape(dps, tokens, vl)]
where the time goes in v2:
time: 37.4 us; the launch traced here: 37.2 us
  Pallas kernels  35.9 us (96%)
  between operations  1.29 us (3%)
    pallas_call x1, Pallas kernels, on_device(): pl.pallas_call(functools.partial(kernel, shape, chunks), out_shape=(jax.S...  33.5 us
    pallas_call x1, Pallas kernels, on_device(): pl.pallas_call(finish, out_shape=(jax.ShapeDtypeStruct((ks, dv), f32), ja...  2.37 us

profile of v2, /device:TPU:0, one launch (start us, length us, event | category | flops | bytes accessed | tf_op | source)
XLA Modules:
  0.0 37.2 jit_solution(11555368442301298788)
XLA Ops:
  1.3 33.5 %shard_map.140 = (f32[256,1024]{1,0:T(8,128)}, f32[32,4096]{1,0:T(8,128)}, f32[32,128]{1,0:T(8,128)}) custom-call(bf16[16,2048]{1,0:T(8,128)(2,1)} %bitcast.17, f32[1,2048]{1,0:T(1,128)} %norm_gain.1, bf16[2048,256]{1,0:T(8,128)(2,1)} %bitcast.11, bf16[2048,256]{1,0:T(8,128)(2,1)} %bitcast.12, bf16[2048,256]{1,0:T(8,128)(2,1)} %bitcast.13, ...), custom_call_target="tpu_custom_call" | custom-call | tf_op jit(solution)/shard_map/pallas_call | solution.py:324
  34.8 2.4 %shard_map.141 = (f32[256,1024]{1,0:T(8,128)}, f32[32,4096]{1,0:T(8,128)}) custom-call(f32[256,1024]{1,0:T(8,128)} %get-tuple-element.7.state_in, f32[32,4096]{1,0:T(8,128)} %get-tuple-element.8.logits_in, f32[32,128]{1,0:T(8,128)} %get-tuple-element.9.total_in), custom_call_target="tpu_custom_call" | custom-call | tf_op jit(solution)/shard_map/pallas_call | solution.py:334
